TPU v7x, 32 devices: a whole 2x2x4 slice. The times are simulated.
32 devices in a mesh: section: 8 (over z, y), fsdp: 4 (over x, core).
Axes of the slice: x: 2, y: 2, z: 4, core: 2. Of those that a mesh axis runs over, the one named last changes fastest.
Arguments:
- source_rows: bfloat16 [3072, 4096], P(('section', 'fsdp')), may hold values from -6 to 6
- target_rows: bfloat16 [1024, 4096], P('section'), may hold values from -6 to 6
- attn_weights: bfloat16 [8, 4, 4096, 3072], P('section', None, None, 'fsdp'), may hold values from -3.76875 to 3.76875
- gains: float32 [8, 4096], P('section'), may hold values from 0.25 to 1.75
- lengths: int32 [8], P('section'), may hold values from 192 to 384
Outputs:
- source_next: bfloat16 [3072, 4096], P(('section', 'fsdp'))
- target_next: bfloat16 [1024, 4096], P('section')
Inputs may be any that keep to these rules, and one draw needn't show every extreme that they name: Keys at positions lengths[s] and beyond are padding.
All inputs are finite; a program needn't handle non-finite values.
Results may differ from a plain program's by a relative error of at most 0.015.
The roundings to bfloat16 on the way count: a program that leaves them out, or rounds other values in their place, can miss the bound.
Values may be sent and summed in bfloat16 or wider, within the bound.
A program may use at most 128 MiB of HBM per device.

v0:
```python
import functools

import jax
import jax.numpy as jnp
from jax import lax
from jax.experimental import pallas as pl
from jax.experimental.pallas import tpu as pltpu
from jax.sharding import PartitionSpec as P

HEAD_DIM = 64
PIECES = 4
GATHER = 4
F32 = jnp.float32
BF16 = jnp.bfloat16


def rms_norm(block, gain):
    wide = block.astype(F32)
    inverse = lax.rsqrt(jnp.mean(wide * wide, axis=-1, keepdims=True) + 1e-06)
    return (wide * inverse * gain).astype(BF16)


def kernel(
    n_sec, n_f, x_ref, y_ref, gain_ref, len_ref, w_hbm, so_hbm, to_hbm,
    xs, ny, w, acc, qkv, ctx, term, prt, sums, rem, own, prt_own, fin, sland,
    dterm, dprt, dp, yfin, tland,
    w_sem, ag_s, ag_r, pt_s, pt_r, fw_s, fw_r, t1_s, t1_r, x1_s, x1_r,
    t2_s, t2_r, d1_s, d1_r, d2_s, d2_r, ss_s, ss_r, ts_s, ts_r, tf_s, tf_r, o_sem,
):
    chips = n_f // 2
    rows, d = x_ref.shape
    pair = 2 * rows
    total = pair * chips
    t_rows = y_ref.shape[0]
    t_half = t_rows // 2
    width = w.shape[2]
    cn, gn = d // PIECES, d // GATHER
    sec, f = lax.axis_index("section"), lax.axis_index("fsdp")
    core, chip = lax.rem(f, 2), f // 2
    other = 1 - core
    enc = sec < n_sec // 2
    partner = {"fsdp": chip * 2 + other}
    nxt = {"section": lax.rem(sec + 1, n_sec)}
    prv = {"section": lax.rem(sec + n_sec - 1, n_sec)}

    def ahead(k):
        return lax.rem(chip + k, chips)

    def behind(k):
        return lax.rem(chip + chips - k, chips)

    def peer(h):
        return {"fsdp": h * 2 + core}

    def remote(src, dst, send, recv, dev):
        return pltpu.make_async_remote_copy(
            src_ref=src, dst_ref=dst, send_sem=send, recv_sem=recv,
            device_id=dev, device_id_type=pl.DeviceIdType.MESH,
        )

    def at(start, size):
        return pl.ds(pl.multiple_of(start, 16), size)

    def cols(j):
        return pl.ds(j * cn, cn)

    barrier = pltpu.get_barrier_semaphore()
    greet = [partner, nxt, prv] + [peer(ahead(k)) for k in range(1, chips)]
    for dev in greet:
        pl.semaphore_signal(barrier, inc=1, device_id=dev, device_id_type=pl.DeviceIdType.MESH)

    w_copies = [pltpu.make_async_copy(w_hbm.at[0, i], w.at[i], w_sem.at[i]) for i in range(4)]
    for cp in w_copies:
        cp.start()
    gain = gain_ref[...]

    def norm_rows(src, dst, dst_start, count):
        size = 32 if count % 32 == 0 else 16

        def step(r, carry):
            dst[at(dst_start + r * size, size), :] = rms_norm(src[at(r * size, size), :], gain)
            return carry

        lax.fori_loop(0, count // size, step, 0)

    @pl.when(enc)
    def _():
        norm_rows(x_ref, xs, f * rows, rows)

    @pl.when(jnp.logical_not(enc))
    def _():
        xs[at(f * rows, rows), :] = x_ref[...]

    pl.semaphore_wait(barrier, len(greet))

    def block(h, which):
        return at((h * 2 + which) * rows, rows)

    def gather_send(k, j):
        spot = xs.at[block(chip, core), pl.ds(j * gn, gn)]
        return remote(spot, spot, ag_s.at[k - 1, j], ag_r.at[k - 1, j], peer(ahead(k)))

    def gather_recv(k, j):
        spot = xs.at[block(behind(k), core), pl.ds(j * gn, gn)]
        return remote(spot, spot, ag_s.at[k - 1, j], ag_r.at[k - 1, j], peer(behind(k)))

    def forward(k, j, which):
        spot = xs.at[block(behind(k), which), pl.ds(j * gn, gn)]
        return remote(spot, spot, fw_s.at[k - 1, j], fw_r.at[k - 1, j], partner)

    def swap(which):
        spot = xs.at[block(chip, which), :]
        return remote(spot, spot, pt_s, pt_r, partner)

    for j in range(GATHER):
        for k in range(1, chips):
            gather_send(k, j).start()
    swap(core).start()

    def shift_source(j, src):
        return remote(src.at[:, cols(j)], sland.at[:, cols(j)], ss_s.at[j], ss_r.at[j], nxt)

    def half(which):
        return at(which * t_half, t_half)

    def shift_target(j, src):
        return remote(src, tland.at[half(core), cols(j)], ts_s.at[j], ts_r.at[j], nxt)

    @pl.when(enc)
    def _():
        for j in range(PIECES):
            shift_target(j, y_ref.at[half(core), cols(j)]).start()

    @pl.when(jnp.logical_not(enc))
    def _():
        for j in range(PIECES):
            shift_source(j, x_ref).start()

    def project(src, which, start, count):
        qkv[which, at(start, count), :] = jnp.dot(
            src, w[which], preferred_element_type=F32
        ).astype(BF16)

    def project_piece(which, h, j):
        part = jnp.dot(
            xs[at(h * pair, pair), pl.ds(j * gn, gn)], w[which, pl.ds(j * gn, gn), :],
            preferred_element_type=F32,
        )
        if j:
            part = part + acc[which]
        if j < GATHER - 1:
            acc[which] = part
        else:
            qkv[which, at(h * pair, pair), :] = part.astype(BF16)

    @pl.when(jnp.logical_not(enc))
    def _():
        norm_rows(y_ref, ny, 0, t_rows)

    w_copies[0].wait()

    @pl.when(jnp.logical_not(enc))
    def _():
        project(ny[...], 0, 0, t_rows)

    swap(other).wait_recv()

    @pl.when(enc)
    def _():
        project(xs[at(chip * pair, pair), :], 0, chip * pair, pair)

    for which in (1, 2):
        w_copies[which].wait()
        project(xs[at(chip * pair, pair), :], which, chip * pair, pair)

    for k in range(1, chips):
        for j in range(GATHER):
            gather_recv(k, j).wait_recv()
            forward(k, j, core).start()
            forward(k, j, other).wait_recv()

            @pl.when(enc)
            def _():
                project_piece(0, behind(k), j)

            project_piece(1, behind(k), j)
            project_piece(2, behind(k), j)

    length = len_ref[0]

    def attend(start, count):
        key_ok = lax.broadcasted_iota(jnp.int32, (1, total), 1) < length
        first = lax.broadcasted_iota(jnp.int32, (1, 2 * HEAD_DIM), 1) < HEAD_DIM

        def step(t, carry):
            lanes = pl.ds(pl.multiple_of(t * 2 * HEAD_DIM, 128), 2 * HEAD_DIM)
            queries = qkv[0, at(start, count), lanes]
            keys, values = qkv[1, :total, lanes], qkv[2, :total, lanes]
            low = queries * jnp.where(first, 0.125, 0.0).astype(BF16)
            high = queries * jnp.where(first, 0.0, 0.125).astype(BF16)
            scores = lax.dot_general(
                jnp.concatenate([low, high], axis=0), keys, (((1,), (1,)), ((), ())),
                preferred_element_type=F32,
            )
            scores = jnp.where(key_ok, scores, -1000000000.0)
            expo = jnp.exp(scores - jnp.max(scores, axis=-1, keepdims=True))
            soft = (expo * (1.0 / jnp.sum(expo, axis=-1, keepdims=True))).astype(BF16)
            mixed = jnp.dot(soft, values, preferred_element_type=F32)
            ctx[at(start, count), lanes] = jnp.where(
                first, mixed[:count], mixed[count:]
            ).astype(BF16)
            return carry

        lax.fori_loop(0, width // (2 * HEAD_DIM), step, 0)

    on = min(cn, 1024)

    def out_piece(start, count, dst, j):
        def step(t, carry):
            lanes = pl.ds(pl.multiple_of(j * cn + t * on, 128), on)
            dst[:, lanes] = lax.dot_general(
                ctx[at(start, count), :], w[3, lanes, :], (((1,), (1,)), ((), ())),
                preferred_element_type=F32,
            ).astype(BF16)
            return carry

        lax.fori_loop(0, cn // on, step, 0)

    def mate_term(k, j):
        return remote(
            term.at[k - 1, at(other * rows, rows), cols(j)], prt.at[k - 1, :, cols(j)],
            t1_s.at[k - 1, j], t1_r.at[k - 1, j], partner,
        )

    def send_sum(k, j):
        return remote(
            sums.at[k - 1, :, cols(j)], rem.at[k - 1, :, cols(j)],
            x1_s.at[k - 1, j], x1_r.at[k - 1, j], peer(ahead(k)),
        )

    def mate_own(j):
        return remote(
            own.at[at(other * rows, rows), cols(j)], prt_own.at[:, cols(j)],
            t2_s.at[j], t2_r.at[j], partner,
        )

    def mate_target(j):
        return remote(
            dterm.at[half(other), cols(j)], dprt.at[:, cols(j)], d1_s.at[j], d1_r.at[j], partner
        )

    def send_target(k, j):
        return remote(
            dp.at[chip, :, cols(j)], dp.at[chip, :, cols(j)],
            d2_s.at[k - 1, j], d2_r.at[k - 1, j], peer(ahead(k)),
        )

    def recv_target(k, j):
        spot = dp.at[behind(k), :, cols(j)]
        return remote(spot, spot, d2_s.at[k - 1, j], d2_r.at[k - 1, j], peer(behind(k)))

    w_copies[3].wait()

    @pl.when(enc)
    def _():
        for k in range(1, chips):
            start = ahead(k) * pair
            attend(start, pair)

            def pass_on(j):
                mate_term(k, j).wait_recv()
                mine = term[k - 1, at(core * rows, rows), cols(j)].astype(F32)
                sums[k - 1, :, cols(j)] = (mine + prt[k - 1, :, cols(j)].astype(F32)).astype(BF16)
                send_sum(k, j).start()

            for j in range(PIECES):
                out_piece(start, pair, term.at[k - 1], j)
                mate_term(k, j).start()
                if j:
                    pass_on(j - 1)
            pass_on(PIECES - 1)
        attend(chip * pair, pair)
        for j in range(PIECES):
            out_piece(chip * pair, pair, own, j)
            mate_own(j).start()
        for j in range(PIECES):
            mate_own(j).wait_recv()
            delta = own[at(core * rows, rows), cols(j)].astype(F32) + prt_own[:, cols(j)].astype(F32)
            for k in range(1, chips):
                send_sum(k, j).wait_recv()
                delta += rem[k - 1, :, cols(j)].astype(F32)
            fin[:, cols(j)] = (x_ref[:, cols(j)].astype(F32) + delta).astype(BF16)
            shift_source(j, fin).start()
        for j in range(PIECES):
            mate_own(j).wait_send()
            for k in range(1, chips):
                mate_term(k, j).wait_send()
                send_sum(k, j).wait_send()

    @pl.when(jnp.logical_not(enc))
    def _():
        attend(0, t_rows)

        def pass_on(j):
            mate_target(j).wait_recv()
            mine = dterm[half(core), cols(j)].astype(F32)
            dp[chip, :, cols(j)] = (mine + dprt[:, cols(j)].astype(F32)).astype(BF16)
            for k in range(1, chips):
                send_target(k, j).start()

        for j in range(PIECES):
            out_piece(0, t_rows, dterm, j)
            mate_target(j).start()
            if j:
                pass_on(j - 1)
        pass_on(PIECES - 1)
        for j in range(PIECES):
            for k in range(1, chips):
                recv_target(k, j).wait_recv()
            delta = dp[0, :, cols(j)].astype(F32)
            for h in range(1, chips):
                delta += dp[h, :, cols(j)].astype(F32)
            yfin[:, cols(j)] = (y_ref[half(core), cols(j)].astype(F32) + delta).astype(BF16)
            shift_target(j, yfin.at[:, cols(j)]).start()
        for j in range(PIECES):
            mate_target(j).wait_send()
            for k in range(1, chips):
                send_target(k, j).wait_send()

    def cross(j, which):
        spot = tland.at[half(which), cols(j)]
        return remote(spot, spot, tf_s.at[j], tf_r.at[j], partner)

    def put_target(j, which, slot):
        return pltpu.make_async_copy(
            tland.at[half(which), cols(j)], to_hbm.at[half(which), cols(j)], o_sem.at[slot, j]
        )

    def put_source(j):
        return pltpu.make_async_copy(sland.at[:, cols(j)], so_hbm.at[:, cols(j)], o_sem.at[2, j])

    for j in range(PIECES):
        shift_target(j, yfin.at[:, cols(j)]).wait_recv()
        cross(j, core).start()
        put_target(j, core, 0).start()
    for j in range(PIECES):
        shift_source(j, fin).wait_recv()
        put_source(j).start()
    for j in range(PIECES):
        cross(j, other).wait_recv()
        put_target(j, other, 1).start()

    swap(core).wait_send()
    for j in range(GATHER):
        for k in range(1, chips):
            gather_send(k, j).wait_send()
            forward(k, j, core).wait_send()
    for j in range(PIECES):
        shift_source(j, fin).wait_send()
        shift_target(j, yfin.at[:, cols(j)]).wait_send()
        cross(j, core).wait_send()
        put_target(j, core, 0).wait()
        put_target(j, other, 1).wait()
        put_source(j).wait()


def local(n_sec, n_f, source_rows, target_rows, attn_weights, gains, lengths):
    chips = n_f // 2
    more = max(chips - 1, 1)
    rows, d = source_rows.shape
    t_rows = target_rows.shape[0]
    width = attn_weights.shape[3]
    pair, total, t_half = 2 * rows, rows * n_f, t_rows // 2
    q_rows = max(total, t_rows)
    dma = pltpu.SemaphoreType.DMA
    vmem = lambda *shape: pltpu.VMEM(shape, BF16)
    scratch = [
        vmem(total, d), vmem(t_rows, d), vmem(4, d, width), pltpu.VMEM((3, pair, width), F32),
        vmem(3, q_rows, width), vmem(q_rows, width),
        vmem(more, pair, d), vmem(more, rows, d), vmem(more, rows, d), vmem(more, rows, d),
        vmem(pair, d), vmem(rows, d), vmem(rows, d), vmem(rows, d),
        vmem(t_rows, d), vmem(t_half, d), vmem(chips, t_half, d), vmem(t_half, d), vmem(t_rows, d),
        dma((4,)), dma((more, GATHER)), dma((more, GATHER)), dma, dma,
        dma((more, GATHER)), dma((more, GATHER)),
        dma((more, PIECES)), dma((more, PIECES)), dma((more, PIECES)), dma((more, PIECES)),
        dma((PIECES,)), dma((PIECES,)), dma((PIECES,)), dma((PIECES,)),
        dma((more, PIECES)), dma((more, PIECES)),
        dma((PIECES,)), dma((PIECES,)), dma((PIECES,)), dma((PIECES,)), dma((PIECES,)), dma((PIECES,)),
        dma((3, PIECES)),
    ]
    in_vmem = pl.BlockSpec(memory_space=pltpu.VMEM)
    anywhere = pl.BlockSpec(memory_space=pl.ANY)
    moved = pl.pallas_call(
        functools.partial(kernel, n_sec, n_f),
        out_shape=(
            pltpu.VMEM(source_rows.shape, BF16),
            pltpu.VMEM(target_rows.shape, BF16),
        ),
        in_specs=[in_vmem, in_vmem, in_vmem, pl.BlockSpec(memory_space=pltpu.SMEM), anywhere],
        out_specs=(anywhere, anywhere),
        scratch_shapes=scratch,
        compiler_params=pltpu.CompilerParams(
            collective_id=0, has_side_effects=True, vmem_limit_bytes=52 * 1024 * 1024
        ),
    )(source_rows, target_rows, gains, lengths, attn_weights)
    return settle(*moved)


def settle(source, target):
    def body(a_ref, b_ref, a_out, b_out, a_vmem, b_vmem, in_sem, out_sem):
        plan = []
        for src, mid, dst in ((a_ref, a_vmem, a_out), (b_ref, b_vmem, b_out)):
            step = src.shape[1] // 4
            for j in range(4):
                lanes = pl.ds(j * step, step)
                n = len(plan)
                plan.append((
                    pltpu.make_async_copy(src.at[:, lanes], mid.at[:, lanes], in_sem.at[n]),
                    pltpu.make_async_copy(mid.at[:, lanes], dst.at[:, lanes], out_sem.at[n]),
                ))
        for into, _ in plan:
            into.start()
        for into, out in plan:
            into.wait()
            out.start()
        for _, out in plan:
            out.wait()

    anywhere = pl.BlockSpec(memory_space=pl.ANY)
    return pl.pallas_call(
        body,
        out_shape=tuple(jax.ShapeDtypeStruct(v.shape, v.dtype) for v in (source, target)),
        in_specs=[anywhere, anywhere],
        out_specs=(anywhere, anywhere),
        scratch_shapes=[
            pltpu.VMEM(source.shape, source.dtype), pltpu.VMEM(target.shape, target.dtype),
            pltpu.SemaphoreType.DMA((8,)), pltpu.SemaphoreType.DMA((8,)),
        ],
        compiler_params=pltpu.CompilerParams(vmem_limit_bytes=8 * 1024 * 1024),
    )(source, target)


def solution(mesh):
    in_specs = (
        P(("section", "fsdp"), None),
        P("section", None),
        P("section", None, None, "fsdp"),
        P("section", None),
        P("section"),
    )
    out_specs = (P(("section", "fsdp"), None), P("section", None))
    body = functools.partial(local, mesh.shape["section"], mesh.shape["fsdp"])
    return jax.shard_map(body, mesh=mesh, in_specs=in_specs, out_specs=out_specs, check_vma=False)
```

profile of v0, /device:TPU:0, one launch (start us, length us, event | category | flops | bytes accessed | tf_op | source)
XLA Modules:
  0.0 65.4 jit_solution(12141543550491116032)
XLA Ops:
  1.3 0.0 copy-start
  1.3 0.7 %copy-done = f32[1,4096]{1,0:T(1,128)S(1)} copy-done((f32[1,4096]{1,0:T(1,128)S(1)}, f32[1,4096]{1,0:T(1,128)}, u32[]{:S(2)}) %copy-start) | copy-done | bytes 16408
  2.0 61.7 %shard_map.68 = (bf16[96,4096]{1,0:T(8,128)(2,1)S(1)}, bf16[128,4096]{1,0:T(8,128)(2,1)S(1)}) custom-call(bf16[96,4096]{1,0:T(8,128)(2,1)} %x_ref.1, bf16[128,4096]{1,0:T(8,128)(2,1)} %y_ref.1, f32[1,4096]{1,0:T(1,128)S(1)} %copy-done, s32[1]{0:T(128)S(6)} %copy.7.len_ref, bf16[1,4,4096,768]{3,2,1,0:T(8,128)(2,1)} %w_hbm.1), custom_call_target="tpu_custom_call" | custom-call | tf_op jit(solution)/shard_map/pallas_call | solution.py:393
  63.7 1.5 %shard_map.69 = (bf16[96,4096]{1,0:T(8,128)(2,1)}, bf16[128,4096]{1,0:T(8,128)(2,1)}) custom-call(bf16[96,4096]{1,0:T(8,128)(2,1)S(1)} %get-tuple-element.4.a_ref, bf16[128,4096]{1,0:T(8,128)(2,1)S(1)} %get-tuple-element.5.b_ref), custom_call_target="tpu_custom_call" | custom-call | tf_op jit(solution)/shard_map/pallas_call | solution.py:430
Async XLA Ops:
  1.3 0.7 %copy-start = (f32[1,4096]{1,0:T(1,128)S(1)}, f32[1,4096]{1,0:T(1,128)}, u32[]{:S(2)}) copy-start(f32[1,4096]{1,0:T(1,128)} %gain_ref.1) | copy-start | bytes 49156
where the time goes:
time: 65.7 us; the launch traced here: 65.4 us
  Pallas kernels  63.3 us (96%)
  between operations  1.45 us (2%)
  local copies, waits for them, and re-layouts  0.71 us (1%)
    pallas_call x1, Pallas kernels, local(): pl.pallas_call(functools.partial(kernel, n_sec, n_f), out_shape=(pltpu.VM...  61.7 us
    pallas_call x1, Pallas kernels, settle(): pl.pallas_call(body, out_shape=tuple((jax.ShapeDtypeStruct(v.shape, v.dty...  1.55 us

commit v1 on v0

v1 whole, which is shorter than its diff:
```python
import functools
import math

import jax
import jax.numpy as jnp
from jax import lax
from jax.experimental import pallas as pl
from jax.experimental.pallas import tpu as pltpu
from jax.sharding import PartitionSpec as P

HEAD_DIM = 64
BLOCKS = 8
CUTS = 2
GATHER = (2, 2, 2, 2, 2, 2, 1, 1, 1, 1)
LEAD = (("O", 0), ("O", 1), ("O", 2), ("S", 0))
TRAIL = (
    ("S", 1), ("S", 2), ("W", 0), ("W", 1), ("O", 3), ("F", 0), ("O", 4), ("F", 1), ("S", 3),
    ("W", 2), ("F", 2), ("W", 3), ("O", 5), ("S", 4), ("F", 3), ("O", 6), ("W", 4), ("F", 4),
    ("S", 5), ("O", 7), ("F", 5), ("W", 5), ("S", 6), ("F", 6), ("W", 6), ("S", 7), ("F", 7),
    ("W", 7),
) + tuple(("F", j) for j in range(8, BLOCKS * CUTS))
F32 = jnp.float32
BF16 = jnp.bfloat16


def rms_norm(block, gain):
    wide = block.astype(F32)
    inverse = lax.rsqrt(jnp.mean(wide * wide, axis=-1, keepdims=True) + 1e-06)
    return (wide * inverse * gain).astype(BF16)


def spans_of(parts, d):
    unit = d // sum(parts)
    return [(sum(parts[:j]) * unit, part * unit) for j, part in enumerate(parts)]


def chunk_of(count):
    return 32 if count % 32 == 0 else 16


def kernel(
    n_sec, n_f, x_hbm, y_hbm, gain_hbm, len_hbm, w_hbm, so, to,
    xin, yin, gain_ref, len_ref, xs, ny, w, acc, qkv, ctx, term, prt, sums, rem, own, prt_own, fin,
    dterm, dprt, dp, yfin,
    x_sem, y_sem, g_sem, w_sem, ag_s, ag_r, pt_s, pt_r, fw_s, fw_r, t1_s, t1_r, x1_s, x1_r,
    t2_s, t2_r, ss_s, ss_r, ts_s, ts_r, tf_s, tf_r,
):
    chips = n_f // 2
    rows, d = xin.shape
    pair = 2 * rows
    total = pair * chips
    t_rows = yin.shape[0]
    t_half = t_rows // 2
    width = w.shape[2]
    spans = spans_of(GATHER, d)
    n_g, n_p = len(spans), BLOCKS
    cn, fn = d // BLOCKS, d // (BLOCKS * CUTS)
    sec, f = lax.axis_index("section"), lax.axis_index("fsdp")
    core, chip = lax.rem(f, 2), f // 2
    other = 1 - core
    enc = sec < n_sec // 2
    dec = jnp.logical_not(enc)
    partner = {"fsdp": chip * 2 + other}
    nxt = {"section": lax.rem(sec + 1, n_sec)}
    prv = {"section": lax.rem(sec + n_sec - 1, n_sec)}

    def ahead(k):
        return lax.rem(chip + k, chips)

    def behind(k):
        return lax.rem(chip + chips - k, chips)

    def peer(h):
        return {"fsdp": h * 2 + core}

    def remote(src, dst, send, recv, dev):
        return pltpu.make_async_remote_copy(
            src_ref=src, dst_ref=dst, send_sem=send, recv_sem=recv,
            device_id=dev, device_id_type=pl.DeviceIdType.MESH,
        )

    def at(start, size):
        return pl.ds(pl.multiple_of(start, 16), size)

    def cols(j):
        return pl.ds(j * cn, cn)

    def fine(j):
        return pl.ds(j * fn, fn)

    barrier = pltpu.get_barrier_semaphore()
    greet = [partner, prv] + [peer(ahead(k)) for k in range(1, chips)]
    with jax.named_scope("signal"):
        for dev in greet:
            pl.semaphore_signal(barrier, inc=1, device_id=dev, device_id_type=pl.DeviceIdType.MESH)

    x_rows, y_rows = chunk_of(rows), chunk_of(t_rows)
    gain_copy = pltpu.make_async_copy(gain_hbm, gain_ref, g_sem.at[0])
    len_copy = pltpu.make_async_copy(len_hbm, len_ref, g_sem.at[1])
    y_copy = pltpu.make_async_copy(y_hbm, yin, y_sem)
    w_copies = [pltpu.make_async_copy(w_hbm.at[0, i], w.at[i], w_sem.at[i]) for i in range(4)]
    x_copy = pltpu.make_async_copy(x_hbm, xin, x_sem)
    gain_copy.start()
    x_copy.start()
    y_copy.start()
    gain_copy.wait()
    gain = gain_ref[...]
    with jax.named_scope("x_wait"):
        x_copy.wait()
    for cp in w_copies:
        cp.start()
    len_copy.start()

    def block(h, which):
        return at((h * 2 + which) * rows, rows)

    @pl.when(enc)
    def _():
        def step(r, carry):
            xs[at(f * rows + r * x_rows, x_rows), :] = rms_norm(
                xin[at(r * x_rows, x_rows), :], gain
            )
            return carry

        lax.fori_loop(0, rows // x_rows, step, 0)

    @pl.when(dec)
    def _():
        xs[at(f * rows, rows), :] = xin[...]

    with jax.named_scope("barrier_wait"):
        pl.semaphore_wait(barrier, len(greet))

    def gather_send(k, j):
        spot = xs.at[block(chip, core), pl.ds(*spans[j])]
        return remote(spot, spot, ag_s.at[k - 1], ag_r.at[k - 1, j], peer(ahead(k)))

    def gather_recv(k, j):
        spot = xs.at[block(behind(k), core), pl.ds(*spans[j])]
        return remote(spot, spot, ag_s.at[k - 1], ag_r.at[k - 1, j], peer(behind(k)))

    def forward(k, j, which):
        spot = xs.at[block(behind(k), which), pl.ds(*spans[j])]
        return remote(spot, spot, fw_s.at[k - 1], fw_r.at[k - 1, j], partner)

    def swap(which):
        spot = xs.at[block(chip, which), :]
        return remote(spot, spot, pt_s, pt_r, partner)

    for j in range(n_g):
        for k in range(1, chips):
            gather_send(k, j).start()
    swap(core).start()

    def shift_source(j, src):
        return remote(src.at[:, fine(j)], so.at[:, fine(j)], ss_s, ss_r, nxt)

    def half(which):
        return at(which * t_half, t_half)

    def shift_target(j, src):
        return remote(src, to.at[half(core), cols(j)], ts_s, ts_r.at[j], nxt)

    with jax.named_scope("y_wait"):
        y_copy.wait()

    @pl.when(enc)
    def _():
        for j in range(n_p):
            shift_target(j, yin.at[half(core), cols(j)]).start()

    @pl.when(dec)
    def _():
        for j in range(n_p * CUTS):
            shift_source(j, xin).start()

    scales = (HEAD_DIM**-0.5 * math.log2(math.e), None, None)

    def store(which, start, count, value):
        if scales[which] is not None:
            value = value * scales[which]
        qkv[which, at(start, count), :] = value.astype(BF16)

    def project(src, which, start, count):
        store(which, start, count, jnp.dot(src, w[which], preferred_element_type=F32))

    def project_piece(which, h, j):
        lanes = pl.ds(*spans[j])
        part = jnp.dot(
            xs[at(h * pair, pair), lanes], w[which, lanes, :], preferred_element_type=F32
        )
        if j:
            part = part + acc[which]
        if j < n_g - 1:
            acc[which] = part
        else:
            store(which, h * pair, pair, part)

    @pl.when(dec)
    def _():
        def step(r, carry):
            spot = at(r * y_rows, y_rows)
            ny[spot, :] = rms_norm(yin[spot, :], gain)
            return carry

        lax.fori_loop(0, t_rows // y_rows, step, 0)

    with jax.named_scope("wait_w0"):
        w_copies[0].wait()

    @pl.when(dec)
    def _():
        with jax.named_scope("proj_ny"):
            project(ny[...], 0, 0, t_rows)

    with jax.named_scope("wait_swap"):
        swap(other).wait_recv()

    @pl.when(enc)
    def _():
        with jax.named_scope("proj_q"):
            project(xs[at(chip * pair, pair), :], 0, chip * pair, pair)

    for which in (1, 2):
        with jax.named_scope(f"wait_w{which}"):
            w_copies[which].wait()
        with jax.named_scope(f"proj_{which}"):
            project(xs[at(chip * pair, pair), :], which, chip * pair, pair)

    def consume(k, j):
        with jax.named_scope(f"fwait{j}"):
            forward(k, j, other).wait_recv()

        @pl.when(enc)
        def _():
            with jax.named_scope(f"pp0_{j}"):
                project_piece(0, behind(k), j)

        with jax.named_scope(f"pp12_{j}"):
            project_piece(1, behind(k), j)
            project_piece(2, behind(k), j)

    arrivals = [(k, j) for k in range(1, chips) for j in range(n_g)]
    for n, (k, j) in enumerate(arrivals):
        with jax.named_scope(f"gwait{j}"):
            gather_recv(k, j).wait_recv()
        forward(k, j, core).start()
        if n:
            consume(*arrivals[n - 1])
    if arrivals:
        consume(*arrivals[-1])

    with jax.named_scope("wait_len"):
        len_copy.wait()
    length = len_ref[0]

    def attend(start, count):
        sure = total // 2 // 128 * 128
        key_ok = sure + lax.broadcasted_iota(jnp.int32, (1, total - sure), 1) < length
        first = lax.broadcasted_iota(jnp.int32, (1, 2 * HEAD_DIM), 1) < HEAD_DIM
        ones = jnp.ones((total, 2 * HEAD_DIM), BF16)

        def step(t, carry):
            lanes = pl.ds(pl.multiple_of(t * 2 * HEAD_DIM, 128), 2 * HEAD_DIM)
            queries = qkv[0, at(start, count), lanes]
            keys = qkv[1, :total, lanes]
            values = jnp.concatenate([qkv[2, :total, lanes], ones], axis=1)
            zero = jnp.zeros_like(queries)
            both = jnp.concatenate(
                [jnp.where(first, queries, zero), jnp.where(first, zero, queries)], axis=0
            )
            scores = lax.dot_general(
                both, keys, (((1,), (1,)), ((), ())), preferred_element_type=F32
            )
            tail = jnp.where(key_ok, scores[:, sure:], -1000000000.0 * math.log2(math.e))
            if sure:
                scores = jnp.concatenate([scores[:, :sure], tail], axis=1)
            else:
                scores = tail
            expo = jnp.exp2(scores - jnp.max(scores, axis=-1, keepdims=True)).astype(BF16)
            mixed = jnp.dot(expo, values, preferred_element_type=F32)
            mixed = mixed[:, : 2 * HEAD_DIM] * (1.0 / mixed[:, 2 * HEAD_DIM :])
            ctx[at(start, count), lanes] = jnp.where(
                first, mixed[:count], mixed[count:]
            ).astype(BF16)
            return carry

        with jax.named_scope("attend"):
            lax.fori_loop(0, width // (2 * HEAD_DIM), step, 0, unroll=True)

    def out_piece(start, count, dst, j):
        with jax.named_scope("outp"):
            dst[:, cols(j)] = lax.dot_general(
                ctx[at(start, count), :], w[3, cols(j), :], (((1,), (1,)), ((), ())),
                preferred_element_type=F32,
            ).astype(BF16)

    def mate_term(k, j):
        return remote(
            term.at[k - 1, at(other * rows, rows), cols(j)], prt.at[k - 1, :, cols(j)],
            t1_s.at[k - 1], t1_r.at[k - 1, j], partner,
        )

    def send_sum(k, j):
        return remote(
            sums.at[k - 1, :, fine(j)], rem.at[k - 1, :, fine(j)],
            x1_s.at[k - 1], x1_r.at[k - 1, j], peer(ahead(k)),
        )

    def mate_own(j):
        return remote(
            own.at[at(other * rows, rows), cols(j)], prt_own.at[:, cols(j)],
            t2_s, t2_r.at[j], partner,
        )

    def mate_target(j):
        return remote(
            dterm.at[half(other), cols(j)], dprt.at[:, cols(j)], t1_s.at[0], t1_r.at[0, j], partner
        )

    def send_target(k, j):
        return remote(
            dp.at[chip, :, cols(j)], dp.at[chip, :, cols(j)],
            x1_s.at[k - 1], x1_r.at[k - 1, j], peer(ahead(k)),
        )

    def recv_target(k, j):
        spot = dp.at[behind(k), :, cols(j)]
        return remote(spot, spot, x1_s.at[k - 1], x1_r.at[k - 1, j], peer(behind(k)))

    with jax.named_scope("wait_w3"):
        w_copies[3].wait()

    @pl.when(enc)
    def _():
        def term_piece(k, j):
            out_piece(ahead(k) * pair, pair, term.at[k - 1], j)
            mate_term(k, j).start()

        def pass_on(k, j):
            with jax.named_scope("mtw"):
                mate_term(k, j).wait_recv()
            mine = term[k - 1, at(core * rows, rows), cols(j)].astype(F32)
            sums[k - 1, :, cols(j)] = (mine + prt[k - 1, :, cols(j)].astype(F32)).astype(BF16)
            for cut in range(CUTS):
                send_sum(k, j * CUTS + cut).start()

        def own_piece(j):
            out_piece(chip * pair, pair, own, j)
            mate_own(j).start()

        def finish(j):
            if j % CUTS == 0:
                with jax.named_scope("mow"):
                    mate_own(j // CUTS).wait_recv()
            delta = own[at(core * rows, rows), fine(j)].astype(F32) + prt_own[:, fine(j)].astype(F32)
            for k in range(1, chips):
                with jax.named_scope(f"ssw{j}"):
                    send_sum(k, j).wait_recv()
                delta += rem[k - 1, :, fine(j)].astype(F32)
            fin[:, fine(j)] = (xin[:, fine(j)].astype(F32) + delta).astype(BF16)
            shift_source(j, fin).start()

        for k in range(1, chips - 1):
            attend(ahead(k) * pair, pair)
            for j in range(n_p):
                term_piece(k, j)
                if j:
                    pass_on(k, j - 1)
            pass_on(k, n_p - 1)

        last = chips - 1
        acts = {"O": lambda j: term_piece(last, j), "S": lambda j: pass_on(last, j),
                "W": own_piece, "F": finish}
        if last:
            attend(ahead(last) * pair, pair)
            for name, j in LEAD:
                acts[name](j)
        attend(chip * pair, pair)
        for name, j in TRAIL:
            if last or name in "WF":
                acts[name](j)
        whole = pl.ds(0, rows)
        remote(own.at[whole], prt_own, t2_s, t2_r.at[0], partner).wait_send()
        for k in range(1, chips):
            remote(
                term.at[k - 1, whole], prt.at[k - 1], t1_s.at[k - 1], t1_r.at[k - 1, 0], partner
            ).wait_send()
            remote(
                sums.at[k - 1], rem.at[k - 1], x1_s.at[k - 1], x1_r.at[k - 1, 0], peer(ahead(k))
            ).wait_send()

    @pl.when(dec)
    def _():
        attend(0, t_rows)

        def pass_on(j):
            with jax.named_scope("mtgw"):
                mate_target(j).wait_recv()
            mine = dterm[half(core), cols(j)].astype(F32)
            dp[chip, :, cols(j)] = (mine + dprt[:, cols(j)].astype(F32)).astype(BF16)
            for k in range(1, chips):
                send_target(k, j).start()

        for j in range(n_p):
            out_piece(0, t_rows, dterm, j)
            mate_target(j).start()
            if j > 2:
                pass_on(j - 3)
        for j in range(n_p - 3, n_p):
            pass_on(j)
        for j in range(n_p):
            for k in range(1, chips):
                with jax.named_scope(f"rtw{j}"):
                    recv_target(k, j).wait_recv()
            delta = dp[0, :, cols(j)].astype(F32)
            for h in range(1, chips):
                delta += dp[h, :, cols(j)].astype(F32)
            yfin[:, cols(j)] = (yin[half(core), cols(j)].astype(F32) + delta).astype(BF16)
            shift_target(j, yfin.at[:, cols(j)]).start()
        remote(dterm.at[half(other)], dprt, t1_s.at[0], t1_r.at[0, 0], partner).wait_send()
        for k in range(1, chips):
            remote(
                dp.at[chip], dp.at[chip], x1_s.at[k - 1], x1_r.at[k - 1, 0], peer(ahead(k))
            ).wait_send()

    def cross(which, lanes):
        spot = to.at[half(which), lanes]
        return remote(spot, spot, tf_s, tf_r, partner)

    for j in range(n_p):
        with jax.named_scope(f"stw{j}"):
            shift_target(j, yfin.at[:, cols(j)]).wait_recv()
        cross(core, cols(j)).start()
    every = pl.ds(0, d)
    shifted = remote(fin, so, ss_s, ss_r, nxt)
    with jax.named_scope("shw"):
        shifted.wait_recv()
    with jax.named_scope("crw"):
        cross(other, every).wait_recv()

    with jax.named_scope("end"):
        swap(core).wait_send()
        for k in range(1, chips):
            mine, theirs = xs.at[block(chip, core)], xs.at[block(behind(k), core)]
            remote(mine, mine, ag_s.at[k - 1], ag_r.at[k - 1, 0], peer(ahead(k))).wait_send()
            remote(theirs, theirs, fw_s.at[k - 1], fw_r.at[k - 1, 0], partner).wait_send()
        shifted.wait_send()
        remote(yfin, to.at[half(core)], ts_s, ts_r.at[0], nxt).wait_send()
        cross(core, every).wait_send()


def local(n_sec, n_f, source_rows, target_rows, attn_weights, gains, lengths):
    chips = n_f // 2
    more = max(chips - 1, 1)
    rows, d = source_rows.shape
    t_rows = target_rows.shape[0]
    width = attn_weights.shape[3]
    pair, total, t_half = 2 * rows, rows * n_f, t_rows // 2
    q_rows = max(total, t_rows)
    n_g, n_p = len(GATHER), BLOCKS
    dma = pltpu.SemaphoreType.DMA
    vmem = lambda *shape: pltpu.VMEM(shape, BF16)
    scratch = [
        vmem(rows, d), vmem(t_rows, d), pltpu.VMEM((1, d), F32), pltpu.SMEM((1,), jnp.int32),
        vmem(total, d), vmem(t_rows, d), vmem(4, d, width), pltpu.VMEM((3, pair, width), F32),
        vmem(3, q_rows, width), vmem(q_rows, width),
        vmem(more, pair, d), vmem(more, rows, d), vmem(more, rows, d), vmem(more, rows, d),
        vmem(pair, d), vmem(rows, d), vmem(rows, d),
        vmem(t_rows, d), vmem(t_half, d), vmem(chips, t_half, d), vmem(t_half, d),
        dma, dma, dma((2,)),
        dma((4,)), dma((more,)), dma((more, n_g)), dma, dma, dma((more,)), dma((more, n_g)),
        dma((more,)), dma((more, n_p)), dma((more,)), dma((more, n_p * CUTS)), dma, dma((n_p,)),
        dma, dma, dma, dma((n_p,)), dma, dma,
    ]
    anywhere = pl.BlockSpec(memory_space=pl.ANY)
    moved = pl.pallas_call(
        functools.partial(kernel, n_sec, n_f),
        out_shape=(
            pltpu.VMEM(source_rows.shape, BF16),
            pltpu.VMEM(target_rows.shape, BF16),
        ),
        in_specs=[anywhere] * 5,
        out_specs=(anywhere, anywhere),
        scratch_shapes=scratch,
        compiler_params=pltpu.CompilerParams(
            collective_id=0, has_side_effects=True, vmem_limit_bytes=56 * 1024 * 1024
        ),
    )(source_rows, target_rows, gains, lengths, attn_weights)
    return settle(*moved)


def settle(source, target):
    def body(a_ref, b_ref, a_out, b_out, sem):
        plan = []
        for src, dst in ((a_ref, a_out), (b_ref, b_out)):
            step = src.shape[1] // 4
            for j in range(4):
                lanes = pl.ds(j * step, step)
                plan.append(pltpu.make_async_copy(src.at[:, lanes], dst.at[:, lanes], sem.at[len(plan)]))
        for copy in plan:
            copy.start()
        for copy in plan:
            copy.wait()

    anywhere = pl.BlockSpec(memory_space=pl.ANY)
    return pl.pallas_call(
        body,
        out_shape=tuple(jax.ShapeDtypeStruct(v.shape, v.dtype) for v in (source, target)),
        in_specs=[anywhere, anywhere],
        out_specs=(anywhere, anywhere),
        scratch_shapes=[pltpu.SemaphoreType.DMA((8,))],
        compiler_params=pltpu.CompilerParams(vmem_limit_bytes=8 * 1024 * 1024),
    )(source, target)


def solution(mesh):
    in_specs = (
        P(("section", "fsdp"), None),
        P("section", None),
        P("section", None, None, "fsdp"),
        P("section", None),
        P("section"),
    )
    out_specs = (P(("section", "fsdp"), None), P("section", None))
    body = functools.partial(local, mesh.shape["section"], mesh.shape["fsdp"])
    return jax.shard_map(body, mesh=mesh, in_specs=in_specs, out_specs=out_specs, check_vma=False)
```

time: 65.7 us -> 52.1 us (0.79)
  Pallas kernels: 63.3 us -> 50 us
  local copies, waits for them, and re-layouts: 0.71 us -> 0 us
    pallas_call x1, Pallas kernels: 61.7 us -> 48.7 us  [local(): pl.pallas_call(functools.partial(kernel, n_sec, n_f), out_shape=(pltpu.VM...]
    unnamed x2 -> x0, local copies, waits for them, and re-layouts: 0.71 us -> none
where the time goes in v1:
time: 52.1 us; the launch traced here: 51.5 us
  Pallas kernels  50 us (96%)
  between operations  1.45 us (3%)
    pallas_call x1, Pallas kernels, local(): pl.pallas_call(functools.partial(kernel, n_sec, n_f), out_shape=(pltpu.VM...  48.7 us
    pallas_call x1, Pallas kernels, settle(): pl.pallas_call(body, out_shape=tuple((jax.ShapeDtypeStruct(v.shape, v.dty...  1.29 us

profile of v1, /device:TPU:0, one launch (start us, length us, event | category | flops | bytes accessed | tf_op | source)
XLA Modules:
  0.0 51.5 jit_solution(5415730999685883755)
XLA Ops:
  1.3 48.7 %shard_map.68 = (bf16[96,4096]{1,0:T(8,128)(2,1)S(1)}, bf16[128,4096]{1,0:T(8,128)(2,1)S(1)}) custom-call(bf16[96,4096]{1,0:T(8,128)(2,1)} %x_hbm.1, bf16[128,4096]{1,0:T(8,128)(2,1)} %y_hbm.1, f32[1,4096]{1,0:T(1,128)} %gain_hbm.1, s32[1]{0:T(128)S(6)} %copy.7.len_hbm, bf16[1,4,4096,768]{3,2,1,0:T(8,128)(2,1)} %w_hbm.1), custom_call_target="tpu_custom_call" | custom-call | tf_op jit(solution)/shard_map/pallas_call | solution.py:477
  50.0 1.3 %shard_map.69 = (bf16[96,4096]{1,0:T(8,128)(2,1)}, bf16[128,4096]{1,0:T(8,128)(2,1)}) custom-call(bf16[96,4096]{1,0:T(8,128)(2,1)S(1)} %get-tuple-element.4.a_ref, bf16[128,4096]{1,0:T(8,128)(2,1)S(1)} %get-tuple-element.5.b_ref), custom_call_target="tpu_custom_call" | custom-call | tf_op jit(solution)/shard_map/pallas_call | solution.py:507

commit v2 on v1

--- a/solution.py
+++ b/solution.py
@@ -10,15 +10,16 @@
 
 HEAD_DIM = 64
 BLOCKS = 8
-CUTS = 2
-GATHER = (2, 2, 2, 2, 2, 2, 1, 1, 1, 1)
-LEAD = (("O", 0), ("O", 1), ("O", 2), ("S", 0))
+CUTS = (4,) + (2,) * (BLOCKS - 1)
+GATHER = (4, 2, 2, 2, 2, 1, 1, 1, 1)
+MOVED = 2
+LEAD = (("O", 1), ("S", 0))
 TRAIL = (
-    ("S", 1), ("S", 2), ("W", 0), ("W", 1), ("O", 3), ("F", 0), ("O", 4), ("F", 1), ("S", 3),
-    ("W", 2), ("F", 2), ("W", 3), ("O", 5), ("S", 4), ("F", 3), ("O", 6), ("W", 4), ("F", 4),
-    ("S", 5), ("O", 7), ("F", 5), ("W", 5), ("S", 6), ("F", 6), ("W", 6), ("S", 7), ("F", 7),
-    ("W", 7),
-) + tuple(("F", j) for j in range(8, BLOCKS * CUTS))
+    ("S", 1), ("O", 2), ("F", 0), ("W", 1), ("F", 1), ("O", 3), ("F", 2), ("F", 3), ("S", 2),
+    ("O", 4), ("W", 2), ("S", 3), ("F", 4), ("O", 5), ("F", 5), ("W", 3), ("S", 4), ("F", 6),
+    ("O", 6), ("F", 7), ("S", 5), ("W", 4), ("F", 8), ("O", 7), ("F", 9), ("S", 6), ("W", 5),
+    ("F", 10), ("W", 6), ("F", 11), ("S", 7), ("F", 12), ("W", 7),
+) + tuple(("F", j) for j in range(13, sum(CUTS)))
 F32 = jnp.float32
 BF16 = jnp.bfloat16
 
@@ -42,7 +43,7 @@
     n_sec, n_f, x_hbm, y_hbm, gain_hbm, len_hbm, w_hbm, so, to,
     xin, yin, gain_ref, len_ref, xs, ny, w, acc, qkv, ctx, term, prt, sums, rem, own, prt_own, fin,
     dterm, dprt, dp, yfin,
-    x_sem, y_sem, g_sem, w_sem, ag_s, ag_r, pt_s, pt_r, fw_s, fw_r, t1_s, t1_r, x1_s, x1_r,
+    x_sem, y_sem, g_sem, w_sem, ag_s, ag_r, pt_s, pt_r, fw_s, fw_r, mv_s, t1_s, t1_r, x1_s, x1_r,
     t2_s, t2_r, ss_s, ss_r, ts_s, ts_r, tf_s, tf_r,
 ):
     chips = n_f // 2
@@ -54,11 +55,13 @@
     width = w.shape[2]
     spans = spans_of(GATHER, d)
     n_g, n_p = len(spans), BLOCKS
-    cn, fn = d // BLOCKS, d // (BLOCKS * CUTS)
+    cn = d // BLOCKS
+    cuts = [(b, c) for b in range(BLOCKS) for c in range(CUTS[b])]
     sec, f = lax.axis_index("section"), lax.axis_index("fsdp")
     core, chip = lax.rem(f, 2), f // 2
     other = 1 - core
     enc = sec < n_sec // 2
+    even, odd = core == 0, core == 1
     dec = jnp.logical_not(enc)
     partner = {"fsdp": chip * 2 + other}
     nxt = {"section": lax.rem(sec + 1, n_sec)}
@@ -86,7 +89,8 @@
         return pl.ds(j * cn, cn)
 
     def fine(j):
-        return pl.ds(j * fn, fn)
+        b, c = cuts[j]
+        return pl.ds(b * cn + c * (cn // CUTS[b]), cn // CUTS[b])
 
     barrier = pltpu.get_barrier_semaphore()
     greet = [partner, prv] + [peer(ahead(k)) for k in range(1, chips)]
@@ -99,33 +103,41 @@
     len_copy = pltpu.make_async_copy(len_hbm, len_ref, g_sem.at[1])
     y_copy = pltpu.make_async_copy(y_hbm, yin, y_sem)
     w_copies = [pltpu.make_async_copy(w_hbm.at[0, i], w.at[i], w_sem.at[i]) for i in range(4)]
-    x_copy = pltpu.make_async_copy(x_hbm, xin, x_sem)
+    x_copies = [
+        pltpu.make_async_copy(
+            x_hbm.at[pl.ds(r * x_rows, x_rows)], xin.at[pl.ds(r * x_rows, x_rows)], x_sem.at[r]
+        )
+        for r in range(rows // x_rows)
+    ]
     gain_copy.start()
-    x_copy.start()
+    for cp in x_copies:
+        cp.start()
     y_copy.start()
     gain_copy.wait()
     gain = gain_ref[...]
-    with jax.named_scope("x_wait"):
-        x_copy.wait()
-    for cp in w_copies:
-        cp.start()
-    len_copy.start()
+
+    def arrived(r):
+        x_copies[r].wait()
+        if r == len(x_copies) - 1:
+            for cp in w_copies:
+                cp.start()
+            len_copy.start()
 
     def block(h, which):
         return at((h * 2 + which) * rows, rows)
 
     @pl.when(enc)
     def _():
-        def step(r, carry):
+        for r in range(len(x_copies)):
+            arrived(r)
             xs[at(f * rows + r * x_rows, x_rows), :] = rms_norm(
-                xin[at(r * x_rows, x_rows), :], gain
+                xin[pl.ds(r * x_rows, x_rows), :], gain
             )
-            return carry
-
-        lax.fori_loop(0, rows // x_rows, step, 0)
 
     @pl.when(dec)
     def _():
+        for r in range(len(x_copies)):
+            arrived(r)
         xs[at(f * rows, rows), :] = xin[...]
 
     with jax.named_scope("barrier_wait"):
@@ -143,11 +155,24 @@
         spot = xs.at[block(behind(k), which), pl.ds(*spans[j])]
         return remote(spot, spot, fw_s.at[k - 1], fw_r.at[k - 1, j], partner)
 
+    def moved_send(k, j):
+        spot = xs.at[at(chip * pair, pair), pl.ds(*spans[j])]
+        return remote(spot, spot, mv_s.at[0], ag_r.at[k - 1, j], peer(ahead(k)))
+
+    def moved_recv(k, j):
+        spot = xs.at[at(behind(k) * pair, pair), pl.ds(*spans[j])]
+        return remote(spot, spot, mv_s.at[0], ag_r.at[k - 1, j], peer(behind(k)))
+
+    def moved_forward(k, j):
+        spot = xs.at[at(behind(k) * pair, pair), pl.ds(*spans[j])]
+        return remote(spot, spot, mv_s.at[1], fw_r.at[k - 1, j], partner)
+
     def swap(which):
         spot = xs.at[block(chip, which), :]
         return remote(spot, spot, pt_s, pt_r, partner)
 
-    for j in range(n_g):
+    kept = n_g - MOVED
+    for j in range(kept):
         for k in range(1, chips):
             gather_send(k, j).start()
     swap(core).start()
@@ -159,7 +184,7 @@
         return at(which * t_half, t_half)
 
     def shift_target(j, src):
-        return remote(src, to.at[half(core), cols(j)], ts_s, ts_r.at[j], nxt)
+        return remote(src, to.at[half(core), cols(j)], ts_s, ts_r.at[j // (n_p // 2)], nxt)
 
     with jax.named_scope("y_wait"):
         y_copy.wait()
@@ -171,7 +196,7 @@
 
     @pl.when(dec)
     def _():
-        for j in range(n_p * CUTS):
+        for j in range(len(cuts)):
             shift_source(j, xin).start()
 
     scales = (HEAD_DIM**-0.5 * math.log2(math.e), None, None)
@@ -184,14 +209,14 @@
     def project(src, which, start, count):
         store(which, start, count, jnp.dot(src, w[which], preferred_element_type=F32))
 
-    def project_piece(which, h, j):
-        lanes = pl.ds(*spans[j])
+    def project_piece(which, h, group):
+        lanes = pl.ds(spans[group[0]][0], sum(spans[j][1] for j in group))
         part = jnp.dot(
             xs[at(h * pair, pair), lanes], w[which, lanes, :], preferred_element_type=F32
         )
-        if j:
+        if group[0]:
             part = part + acc[which]
-        if j < n_g - 1:
+        if group[-1] < n_g - 1:
             acc[which] = part
         else:
             store(which, h * pair, pair, part)
@@ -215,6 +240,12 @@
 
     with jax.named_scope("wait_swap"):
         swap(other).wait_recv()
+
+    @pl.when(odd)
+    def _():
+        for j in range(kept, n_g):
+            for k in range(1, chips):
+                moved_send(k, j).start()
 
     @pl.when(enc)
     def _():
@@ -227,28 +258,49 @@
         with jax.named_scope(f"proj_{which}"):
             project(xs[at(chip * pair, pair), :], which, chip * pair, pair)
 
-    def consume(k, j):
-        with jax.named_scope(f"fwait{j}"):
-            forward(k, j, other).wait_recv()
+    def consume(k, *group):
+        for j in group:
+            with jax.named_scope(f"fwait{j}"):
+                if j < kept:
+                    forward(k, j, other).wait_recv()
+                else:
+                    @pl.when(even)
+                    def _():
+                        moved_forward(k, j).wait_recv()
 
         @pl.when(enc)
         def _():
             with jax.named_scope(f"pp0_{j}"):
-                project_piece(0, behind(k), j)
+                project_piece(0, behind(k), group)
 
         with jax.named_scope(f"pp12_{j}"):
-            project_piece(1, behind(k), j)
-            project_piece(2, behind(k), j)
-
-    arrivals = [(k, j) for k in range(1, chips) for j in range(n_g)]
-    for n, (k, j) in enumerate(arrivals):
+            project_piece(1, behind(k), group)
+            project_piece(2, behind(k), group)
+
+    def receive(k, j):
         with jax.named_scope(f"gwait{j}"):
-            gather_recv(k, j).wait_recv()
-        forward(k, j, core).start()
-        if n:
-            consume(*arrivals[n - 1])
-    if arrivals:
-        consume(*arrivals[-1])
+            if j < kept:
+                gather_recv(k, j).wait_recv()
+                forward(k, j, core).start()
+            else:
+                @pl.when(odd)
+                def _():
+                    moved_recv(k, j).wait_recv()
+                    moved_forward(k, j).start()
+
+    for k in range(1, chips):
+        for j in range(kept - 1):
+            receive(k, j)
+            if j:
+                consume(k, j - 1)
+        receive(k, kept - 1)
+        receive(k, kept)
+        consume(k, kept - 2)
+        for j in range(kept + 1, n_g):
+            receive(k, j)
+        consume(k, kept - 1, kept)
+        for j in range(kept + 1, n_g):
+            consume(k, j)
 
     with jax.named_scope("wait_len"):
         len_copy.wait()
@@ -260,33 +312,40 @@
         first = lax.broadcasted_iota(jnp.int32, (1, 2 * HEAD_DIM), 1) < HEAD_DIM
         ones = jnp.ones((total, 2 * HEAD_DIM), BF16)
 
-        def step(t, carry):
-            lanes = pl.ds(pl.multiple_of(t * 2 * HEAD_DIM, 128), 2 * HEAD_DIM)
+        def score(t):
+            lanes = pl.ds(t * 2 * HEAD_DIM, 2 * HEAD_DIM)
             queries = qkv[0, at(start, count), lanes]
-            keys = qkv[1, :total, lanes]
-            values = jnp.concatenate([qkv[2, :total, lanes], ones], axis=1)
             zero = jnp.zeros_like(queries)
             both = jnp.concatenate(
                 [jnp.where(first, queries, zero), jnp.where(first, zero, queries)], axis=0
             )
-            scores = lax.dot_general(
-                both, keys, (((1,), (1,)), ((), ())), preferred_element_type=F32
+            return lax.dot_general(
+                both, qkv[1, :total, lanes], (((1,), (1,)), ((), ())), preferred_element_type=F32
             )
+
+        def weigh(scores):
             tail = jnp.where(key_ok, scores[:, sure:], -1000000000.0 * math.log2(math.e))
             if sure:
                 scores = jnp.concatenate([scores[:, :sure], tail], axis=1)
             else:
                 scores = tail
-            expo = jnp.exp2(scores - jnp.max(scores, axis=-1, keepdims=True)).astype(BF16)
+            return jnp.exp2(scores - jnp.max(scores, axis=-1, keepdims=True)).astype(BF16)
+
+        def mix(t, expo):
+            lanes = pl.ds(t * 2 * HEAD_DIM, 2 * HEAD_DIM)
+            values = jnp.concatenate([qkv[2, :total, lanes], ones], axis=1)
             mixed = jnp.dot(expo, values, preferred_element_type=F32)
             mixed = mixed[:, : 2 * HEAD_DIM] * (1.0 / mixed[:, 2 * HEAD_DIM :])
             ctx[at(start, count), lanes] = jnp.where(
                 first, mixed[:count], mixed[count:]
             ).astype(BF16)
-            return carry
 
         with jax.named_scope("attend"):
-            lax.fori_loop(0, width // (2 * HEAD_DIM), step, 0, unroll=True)
+            pairs = range(width // (2 * HEAD_DIM))
+            scores = [score(t) for t in pairs]
+            weights = [weigh(block) for block in scores]
+            for t in pairs:
+                mix(t, weights[t])
 
     def out_piece(start, count, dst, j):
         with jax.named_scope("outp"):
@@ -342,17 +401,18 @@
                 mate_term(k, j).wait_recv()
             mine = term[k - 1, at(core * rows, rows), cols(j)].astype(F32)
             sums[k - 1, :, cols(j)] = (mine + prt[k - 1, :, cols(j)].astype(F32)).astype(BF16)
-            for cut in range(CUTS):
-                send_sum(k, j * CUTS + cut).start()
+            for piece, (b, _) in enumerate(cuts):
+                if b == j:
+                    send_sum(k, piece).start()
 
         def own_piece(j):
             out_piece(chip * pair, pair, own, j)
             mate_own(j).start()
 
         def finish(j):
-            if j % CUTS == 0:
+            if cuts[j][1] == 0:
                 with jax.named_scope("mow"):
-                    mate_own(j // CUTS).wait_recv()
+                    mate_own(cuts[j][0]).wait_recv()
             delta = own[at(core * rows, rows), fine(j)].astype(F32) + prt_own[:, fine(j)].astype(F32)
             for k in range(1, chips):
                 with jax.named_scope(f"ssw{j}"):
@@ -373,10 +433,20 @@
         acts = {"O": lambda j: term_piece(last, j), "S": lambda j: pass_on(last, j),
                 "W": own_piece, "F": finish}
         if last:
-            attend(ahead(last) * pair, pair)
+            for which in (other, core):
+                start = ahead(last) * pair + which * rows
+                attend(start, rows)
+                out_piece(start, rows, term.at[last - 1, at(which * rows, rows)], 0)
+                if which is other:
+                    mate_term(last, 0).start()
             for name, j in LEAD:
                 acts[name](j)
-        attend(chip * pair, pair)
+        for which in (other, core):
+            start = chip * pair + which * rows
+            attend(start, rows)
+            out_piece(start, rows, own.at[at(which * rows, rows)], 0)
+            if which is other:
+                mate_own(0).start()
         for name, j in TRAIL:
             if last or name in "WF":
                 acts[name](j)
@@ -428,10 +498,11 @@
         spot = to.at[half(which), lanes]
         return remote(spot, spot, tf_s, tf_r, partner)
 
-    for j in range(n_p):
+    for j in range(2):
+        part = pl.ds(j * (d // 2), d // 2)
         with jax.named_scope(f"stw{j}"):
-            shift_target(j, yfin.at[:, cols(j)]).wait_recv()
-        cross(core, cols(j)).start()
+            remote(yfin.at[:, part], to.at[half(core), part], ts_s, ts_r.at[j], nxt).wait_recv()
+        cross(core, part).start()
     every = pl.ds(0, d)
     shifted = remote(fin, so, ss_s, ss_r, nxt)
     with jax.named_scope("shw"):
@@ -442,9 +513,19 @@
     with jax.named_scope("end"):
         swap(core).wait_send()
         for k in range(1, chips):
-            mine, theirs = xs.at[block(chip, core)], xs.at[block(behind(k), core)]
+            sent = pl.ds(0, spans[kept][0])
+            mine, theirs = xs.at[block(chip, core), sent], xs.at[block(behind(k), core), sent]
             remote(mine, mine, ag_s.at[k - 1], ag_r.at[k - 1, 0], peer(ahead(k))).wait_send()
             remote(theirs, theirs, fw_s.at[k - 1], fw_r.at[k - 1, 0], partner).wait_send()
+        if chips > 1:
+            late = pl.ds(0, d - spans[kept][0])
+
+            @pl.when(odd)
+            def _():
+                for way, dev in ((0, peer(ahead(1))), (1, partner)):
+                    spot = xs.at[pl.ds(0, total - pair), late]
+                    remote(spot, spot, mv_s.at[way], fw_r.at[0, 0], dev).wait_send()
+
         shifted.wait_send()
         remote(yfin, to.at[half(core)], ts_s, ts_r.at[0], nxt).wait_send()
         cross(core, every).wait_send()
@@ -468,10 +549,10 @@
         vmem(more, pair, d), vmem(more, rows, d), vmem(more, rows, d), vmem(more, rows, d),
         vmem(pair, d), vmem(rows, d), vmem(rows, d),
         vmem(t_rows, d), vmem(t_half, d), vmem(chips, t_half, d), vmem(t_half, d),
-        dma, dma, dma((2,)),
-        dma((4,)), dma((more,)), dma((more, n_g)), dma, dma, dma((more,)), dma((more, n_g)),
-        dma((more,)), dma((more, n_p)), dma((more,)), dma((more, n_p * CUTS)), dma, dma((n_p,)),
-        dma, dma, dma, dma((n_p,)), dma, dma,
+        dma((rows // chunk_of(rows),)), dma, dma((2,)),
+        dma((4,)), dma((more,)), dma((more, n_g)), dma, dma, dma((more,)), dma((more, n_g)), dma((2,)),
+        dma((more,)), dma((more, n_p)), dma((more,)), dma((more, sum(CUTS))), dma, dma((n_p,)),
+        dma, dma, dma, dma((2,)), dma, dma,
     ]
     anywhere = pl.BlockSpec(memory_space=pl.ANY)
     moved = pl.pallas_call(
@@ -494,10 +575,10 @@
     def body(a_ref, b_ref, a_out, b_out, sem):
         plan = []
         for src, dst in ((a_ref, a_out), (b_ref, b_out)):
-            step = src.shape[1] // 4
-            for j in range(4):
-                lanes = pl.ds(j * step, step)
-                plan.append(pltpu.make_async_copy(src.at[:, lanes], dst.at[:, lanes], sem.at[len(plan)]))
+            step = src.shape[0] // 2
+            for j in range(2):
+                some = pl.ds(j * step, step)
+                plan.append(pltpu.make_async_copy(src.at[some], dst.at[some], sem.at[len(plan)]))
         for copy in plan:
             copy.start()
         for copy in plan:
@@ -509,7 +590,7 @@
         out_shape=tuple(jax.ShapeDtypeStruct(v.shape, v.dtype) for v in (source, target)),
         in_specs=[anywhere, anywhere],
         out_specs=(anywhere, anywhere),
-        scratch_shapes=[pltpu.SemaphoreType.DMA((8,))],
+        scratch_shapes=[pltpu.SemaphoreType.DMA((4,))],
         compiler_params=pltpu.CompilerParams(vmem_limit_bytes=8 * 1024 * 1024),
     )(source, target)
 

time: 52.1 us -> 50 us (0.960)
  Pallas kernels: 50 us -> 48.4 us
    pallas_call x1, Pallas kernels: 48.7 us -> 47.1 us  [local(): pl.pallas_call(functools.partial(kernel, n_sec, n_f), out_shape=(pltpu.VM...]
where the time goes in v2:
time: 50 us; the launch traced here: 49.9 us
  Pallas kernels  48.4 us (97%)
  between operations  1.45 us (3%)
    pallas_call x1, Pallas kernels, local(): pl.pallas_call(functools.partial(kernel, n_sec, n_f), out_shape=(pltpu.VM...  47.1 us
    pallas_call x1, Pallas kernels, settle(): pl.pallas_call(body, out_shape=tuple((jax.ShapeDtypeStruct(v.shape, v.dty...  1.26 us

profile of v2, /device:TPU:0, one launch (start us, length us, event | category | flops | bytes accessed | tf_op | source)
XLA Modules:
  0.0 49.9 jit_solution(15624023684086991104)
XLA Ops:
  1.3 47.1 %shard_map.68 = (bf16[96,4096]{1,0:T(8,128)(2,1)S(1)}, bf16[128,4096]{1,0:T(8,128)(2,1)S(1)}) custom-call(bf16[96,4096]{1,0:T(8,128)(2,1)} %x_hbm.1, bf16[128,4096]{1,0:T(8,128)(2,1)} %y_hbm.1, f32[1,4096]{1,0:T(1,128)} %gain_hbm.1, s32[1]{0:T(128)S(6)} %copy.7.len_hbm, bf16[1,4,4096,768]{3,2,1,0:T(8,128)(2,1)} %w_hbm.1), custom_call_target="tpu_custom_call" | custom-call | tf_op jit(solution)/shard_map/pallas_call | solution.py:558
  48.4 1.3 %shard_map.69 = (bf16[96,4096]{1,0:T(8,128)(2,1)}, bf16[128,4096]{1,0:T(8,128)(2,1)}) custom-call(bf16[96,4096]{1,0:T(8,128)(2,1)S(1)} %get-tuple-element.4.a_ref, bf16[128,4096]{1,0:T(8,128)(2,1)S(1)} %get-tuple-element.5.b_ref), custom_call_target="tpu_custom_call" | custom-call | tf_op jit(solution)/shard_map/pallas_call | solution.py:588

commit v3 on v2

--- a/solution.py
+++ b/solution.py
@@ -11,14 +11,14 @@
 HEAD_DIM = 64
 BLOCKS = 8
 CUTS = (4,) + (2,) * (BLOCKS - 1)
-GATHER = (4, 2, 2, 2, 2, 1, 1, 1, 1)
+GATHER = (4, 4, 2, 2, 1, 1, 1, 1)
 MOVED = 2
-LEAD = (("O", 1), ("S", 0))
+LEAD = (("O", 1), ("S", 0), ("O", 2))
 TRAIL = (
-    ("S", 1), ("O", 2), ("F", 0), ("W", 1), ("F", 1), ("O", 3), ("F", 2), ("F", 3), ("S", 2),
-    ("O", 4), ("W", 2), ("S", 3), ("F", 4), ("O", 5), ("F", 5), ("W", 3), ("S", 4), ("F", 6),
-    ("O", 6), ("F", 7), ("S", 5), ("W", 4), ("F", 8), ("O", 7), ("F", 9), ("S", 6), ("W", 5),
-    ("F", 10), ("W", 6), ("F", 11), ("S", 7), ("F", 12), ("W", 7),
+    ("S", 2), ("W", 1), ("F", 0), ("F", 1), ("O", 3), ("F", 2), ("F", 3), ("W", 2), ("O", 4),
+    ("S", 3), ("F", 4), ("O", 5), ("F", 5), ("S", 4), ("W", 3), ("F", 6), ("O", 6), ("F", 7),
+    ("S", 5), ("W", 4), ("F", 8), ("O", 7), ("F", 9), ("S", 6), ("W", 5), ("F", 10), ("S", 7),
+    ("W", 6), ("F", 11), ("F", 12), ("W", 7),
 ) + tuple(("F", j) for j in range(13, sum(CUTS)))
 F32 = jnp.float32
 BF16 = jnp.bfloat16
@@ -41,10 +41,10 @@
 
 def kernel(
     n_sec, n_f, x_hbm, y_hbm, gain_hbm, len_hbm, w_hbm, so, to,
-    xin, yin, gain_ref, len_ref, xs, ny, w, acc, qkv, ctx, term, prt, sums, rem, own, prt_own, fin,
+    xin, yin, gain_ref, len_ref, xs, ny, w, wt, acc, qkv, ctx, term, prt, sums, rem, own, prt_own, fin,
     dterm, dprt, dp, yfin,
-    x_sem, y_sem, g_sem, w_sem, ag_s, ag_r, pt_s, pt_r, fw_s, fw_r, mv_s, t1_s, t1_r, x1_s, x1_r,
-    t2_s, t2_r, ss_s, ss_r, ts_s, ts_r, tf_s, tf_r,
+    load, ag_s, ag_r, pt_s, pt_r, fw_s, fw_r, mv_s, t1_s, x1_s, x1_r,
+    t2_s, ss_s, ss_r, ts_s, ts_r, tf_s, tf_r,
 ):
     chips = n_f // 2
     rows, d = xin.shape
@@ -99,13 +99,13 @@
             pl.semaphore_signal(barrier, inc=1, device_id=dev, device_id_type=pl.DeviceIdType.MESH)
 
     x_rows, y_rows = chunk_of(rows), chunk_of(t_rows)
-    gain_copy = pltpu.make_async_copy(gain_hbm, gain_ref, g_sem.at[0])
-    len_copy = pltpu.make_async_copy(len_hbm, len_ref, g_sem.at[1])
-    y_copy = pltpu.make_async_copy(y_hbm, yin, y_sem)
-    w_copies = [pltpu.make_async_copy(w_hbm.at[0, i], w.at[i], w_sem.at[i]) for i in range(4)]
+    gain_copy = pltpu.make_async_copy(gain_hbm, gain_ref, load.at[4])
+    len_copy = pltpu.make_async_copy(len_hbm, len_ref, load.at[5])
+    y_copy = pltpu.make_async_copy(y_hbm, yin, load.at[6])
+    w_copies = [pltpu.make_async_copy(w_hbm.at[0, i], w.at[i], load.at[i]) for i in range(4)]
     x_copies = [
         pltpu.make_async_copy(
-            x_hbm.at[pl.ds(r * x_rows, x_rows)], xin.at[pl.ds(r * x_rows, x_rows)], x_sem.at[r]
+            x_hbm.at[pl.ds(r * x_rows, x_rows)], xin.at[pl.ds(r * x_rows, x_rows)], load.at[7 + r]
         )
         for r in range(rows // x_rows)
     ]
@@ -126,6 +126,17 @@
     def block(h, which):
         return at((h * 2 + which) * rows, rows)
 
+    def entered():
+        pl.semaphore_wait(barrier, len(greet))
+
+    kept = n_g - MOVED
+
+    def send_rows(r):
+        some = at(f * rows + r * x_rows, x_rows)
+        for k in range(1, chips):
+            spot = xs.at[some, pl.ds(*spans[0])]
+            remote(spot, spot, ag_s.at[k - 1], ag_r.at[k - 1, 0], peer(ahead(k))).start()
+
     @pl.when(enc)
     def _():
         for r in range(len(x_copies)):
@@ -133,15 +144,18 @@
             xs[at(f * rows + r * x_rows, x_rows), :] = rms_norm(
                 xin[pl.ds(r * x_rows, x_rows), :], gain
             )
+            if r == 0:
+                entered()
+            send_rows(r)
 
     @pl.when(dec)
     def _():
         for r in range(len(x_copies)):
             arrived(r)
         xs[at(f * rows, rows), :] = xin[...]
-
-    with jax.named_scope("barrier_wait"):
-        pl.semaphore_wait(barrier, len(greet))
+        entered()
+        for r in range(len(x_copies)):
+            send_rows(r)
 
     def gather_send(k, j):
         spot = xs.at[block(chip, core), pl.ds(*spans[j])]
@@ -171,8 +185,7 @@
         spot = xs.at[block(chip, which), :]
         return remote(spot, spot, pt_s, pt_r, partner)
 
-    kept = n_g - MOVED
-    for j in range(kept):
+    for j in range(1, kept):
         for k in range(1, chips):
             gather_send(k, j).start()
     swap(core).start()
@@ -257,6 +270,13 @@
             w_copies[which].wait()
         with jax.named_scope(f"proj_{which}"):
             project(xs[at(chip * pair, pair), :], which, chip * pair, pair)
+
+    w_copies[3].wait()
+
+    def flip(blocks):
+        with jax.named_scope("flip"):
+            for j in blocks:
+                wt[:, cols(j)] = w[3, cols(j), :].T
 
     def consume(k, *group):
         for j in group:
@@ -288,11 +308,14 @@
                     moved_recv(k, j).wait_recv()
                     moved_forward(k, j).start()
 
+    flip(range(n_p if chips == 1 else n_p // 2))
     for k in range(1, chips):
         for j in range(kept - 1):
             receive(k, j)
             if j:
                 consume(k, j - 1)
+            if k == 1 and 1 <= j <= 2:
+                flip(range(n_p * (j + 1) // 4, n_p * (j + 2) // 4))
         receive(k, kept - 1)
         receive(k, kept)
         consume(k, kept - 2)
@@ -349,15 +372,14 @@
 
     def out_piece(start, count, dst, j):
         with jax.named_scope("outp"):
-            dst[:, cols(j)] = lax.dot_general(
-                ctx[at(start, count), :], w[3, cols(j), :], (((1,), (1,)), ((), ())),
-                preferred_element_type=F32,
+            dst[:, cols(j)] = jnp.dot(
+                ctx[at(start, count), :], wt[:, cols(j)], preferred_element_type=F32
             ).astype(BF16)
 
     def mate_term(k, j):
         return remote(
             term.at[k - 1, at(other * rows, rows), cols(j)], prt.at[k - 1, :, cols(j)],
-            t1_s.at[k - 1], t1_r.at[k - 1, j], partner,
+            t1_s.at[k - 1], fw_r.at[k - 1, j], partner,
         )
 
     def send_sum(k, j):
@@ -369,12 +391,12 @@
     def mate_own(j):
         return remote(
             own.at[at(other * rows, rows), cols(j)], prt_own.at[:, cols(j)],
-            t2_s, t2_r.at[j], partner,
+            t2_s, load.at[j], partner,
         )
 
     def mate_target(j):
         return remote(
-            dterm.at[half(other), cols(j)], dprt.at[:, cols(j)], t1_s.at[0], t1_r.at[0, j], partner
+            dterm.at[half(other), cols(j)], dprt.at[:, cols(j)], t1_s.at[0], fw_r.at[0, j], partner
         )
 
     def send_target(k, j):
@@ -386,9 +408,6 @@
     def recv_target(k, j):
         spot = dp.at[behind(k), :, cols(j)]
         return remote(spot, spot, x1_s.at[k - 1], x1_r.at[k - 1, j], peer(behind(k)))
-
-    with jax.named_scope("wait_w3"):
-        w_copies[3].wait()
 
     @pl.when(enc)
     def _():
@@ -447,14 +466,16 @@
             out_piece(start, rows, own.at[at(which * rows, rows)], 0)
             if which is other:
                 mate_own(0).start()
+                if last:
+                    pass_on(last, 1)
         for name, j in TRAIL:
             if last or name in "WF":
                 acts[name](j)
         whole = pl.ds(0, rows)
-        remote(own.at[whole], prt_own, t2_s, t2_r.at[0], partner).wait_send()
+        remote(own.at[whole], prt_own, t2_s, load.at[0], partner).wait_send()
         for k in range(1, chips):
             remote(
-                term.at[k - 1, whole], prt.at[k - 1], t1_s.at[k - 1], t1_r.at[k - 1, 0], partner
+                term.at[k - 1, whole], prt.at[k - 1], t1_s.at[k - 1], fw_r.at[k - 1, 0], partner
             ).wait_send()
             remote(
                 sums.at[k - 1], rem.at[k - 1], x1_s.at[k - 1], x1_r.at[k - 1, 0], peer(ahead(k))
@@ -488,7 +509,7 @@
                 delta += dp[h, :, cols(j)].astype(F32)
             yfin[:, cols(j)] = (yin[half(core), cols(j)].astype(F32) + delta).astype(BF16)
             shift_target(j, yfin.at[:, cols(j)]).start()
-        remote(dterm.at[half(other)], dprt, t1_s.at[0], t1_r.at[0, 0], partner).wait_send()
+        remote(dterm.at[half(other)], dprt, t1_s.at[0], fw_r.at[0, 0], partner).wait_send()
         for k in range(1, chips):
             remote(
                 dp.at[chip], dp.at[chip], x1_s.at[k - 1], x1_r.at[k - 1, 0], peer(ahead(k))
@@ -544,14 +565,14 @@
     vmem = lambda *shape: pltpu.VMEM(shape, BF16)
     scratch = [
         vmem(rows, d), vmem(t_rows, d), pltpu.VMEM((1, d), F32), pltpu.SMEM((1,), jnp.int32),
-        vmem(total, d), vmem(t_rows, d), vmem(4, d, width), pltpu.VMEM((3, pair, width), F32),
+        vmem(total, d), vmem(t_rows, d), vmem(4, d, width), vmem(width, d), pltpu.VMEM((3, pair, width), F32),
         vmem(3, q_rows, width), vmem(q_rows, width),
         vmem(more, pair, d), vmem(more, rows, d), vmem(more, rows, d), vmem(more, rows, d),
         vmem(pair, d), vmem(rows, d), vmem(rows, d),
         vmem(t_rows, d), vmem(t_half, d), vmem(chips, t_half, d), vmem(t_half, d),
-        dma((rows // chunk_of(rows),)), dma, dma((2,)),
-        dma((4,)), dma((more,)), dma((more, n_g)), dma, dma, dma((more,)), dma((more, n_g)), dma((2,)),
-        dma((more,)), dma((more, n_p)), dma((more,)), dma((more, sum(CUTS))), dma, dma((n_p,)),
+        dma((max(7 + rows // chunk_of(rows), n_p),)),
+        dma((more,)), dma((more, n_g)), dma, dma, dma((more,)), dma((more, max(n_g, n_p))), dma((2,)),
+        dma((more,)), dma((more,)), dma((more, sum(CUTS))), dma,
         dma, dma, dma, dma((2,)), dma, dma,
     ]
     anywhere = pl.BlockSpec(memory_space=pl.ANY)

time: 50 us -> 50 us (level)
  no operation moved by 1% of the time
where the time goes in v3:
time: 50 us; the launch traced here: 49.7 us
  Pallas kernels  48.3 us (97%)
  between operations  1.45 us (3%)
    pallas_call x1, Pallas kernels, local(): pl.pallas_call(functools.partial(kernel, n_sec, n_f), out_shape=(pltpu.VM...  47 us
    pallas_call x1, Pallas kernels, settle(): pl.pallas_call(body, out_shape=tuple((jax.ShapeDtypeStruct(v.shape, v.dty...  1.26 us

profile of v3, /device:TPU:0, one launch (start us, length us, event | category | flops | bytes accessed | tf_op | source)
XLA Modules:
  0.0 49.7 jit_solution(15305321848669603163)
XLA Ops:
  1.3 47.0 %shard_map.68 = (bf16[96,4096]{1,0:T(8,128)(2,1)S(1)}, bf16[128,4096]{1,0:T(8,128)(2,1)S(1)}) custom-call(bf16[96,4096]{1,0:T(8,128)(2,1)} %x_hbm.1, bf16[128,4096]{1,0:T(8,128)(2,1)} %y_hbm.1, f32[1,4096]{1,0:T(1,128)} %gain_hbm.1, s32[1]{0:T(128)S(6)} %copy.7.len_hbm, bf16[1,4,4096,768]{3,2,1,0:T(8,128)(2,1)} %w_hbm.1), custom_call_target="tpu_custom_call" | custom-call | tf_op jit(solution)/shard_map/pallas_call | solution.py:579
  48.3 1.3 %shard_map.69 = (bf16[96,4096]{1,0:T(8,128)(2,1)}, bf16[128,4096]{1,0:T(8,128)(2,1)}) custom-call(bf16[96,4096]{1,0:T(8,128)(2,1)S(1)} %get-tuple-element.4.a_ref, bf16[128,4096]{1,0:T(8,128)(2,1)S(1)} %get-tuple-element.5.b_ref), custom_call_target="tpu_custom_call" | custom-call | tf_op jit(solution)/shard_map/pallas_call | solution.py:609
